TPU v7x, 32 devices: a whole 2x2x4 slice. The times are simulated.
32 devices in a mesh: rows: 4 (over y, x), keys: 8 (over z, core).
Axes of the slice: x: 2, y: 2, z: 4, core: 2. Of those that a mesh axis runs over, the one named last changes fastest.
Arguments:
- pair_rep: bfloat16 [192, 384, 128], P('rows', 'keys'), may hold values from -6 to 6
- norm_gain: float32 [128], replicated, may hold values from 0.1 to 1.9
- w_query: bfloat16 [128, 128], replicated, may hold values from -0.5 to 0.5
- w_key: bfloat16 [128, 128], replicated, may hold values from -0.5 to 0.5
- w_value: bfloat16 [128, 128], replicated, may hold values from -0.5 to 0.5
- w_gate: bfloat16 [128, 128], replicated, may hold values from -0.5 to 0.5
- w_out: bfloat16 [128, 128], replicated, may hold values from -0.5 to 0.5
- pair_bias: bfloat16 [4, 384, 384], P(None, 'keys', 'rows'), may hold values from -12 to 300
Outputs:
- update: bfloat16 [192, 384, 128], P('rows', 'keys')
All inputs are finite; a program needn't handle non-finite values.
Results may differ from a plain program's by a relative error of at most 0.025.
Values may be sent and summed in bfloat16 or wider, within the bound.
No kernel may reach another device: no remote copies, remote signals or barrier semaphores. Data moves between devices by JAX's collectives and lax.ppermute only.
A program may use at most 128 MiB of HBM per device.

v0:
```python
import functools
import math

import jax
import jax.numpy as jnp
from jax import lax
from jax.experimental import pallas as pl
from jax.experimental.pallas import tpu as pltpu
from jax.sharding import PartitionSpec as P

epsilon = 1e-05
cores = 2

f32 = jnp.float32
bf16 = jnp.bfloat16


def vmem(count):
    return [pl.BlockSpec(memory_space=pltpu.VMEM)] * count


def room(shapes, extra=4):
    size = sum(math.prod(s[:-1]) * max(s[-1], 128) * jnp.dtype(kind).itemsize for s, kind in shapes)
    return pltpu.CompilerParams(vmem_limit_bytes=min(size + extra * 2**20, 60 * 2**20))


def kinds(*arrays):
    return [(a.shape, a.dtype) for a in arrays]


def estimate(flops, size):
    return pl.CostEstimate(flops=flops, bytes_accessed=size, transcendentals=0)


def prepare_kernel(chips, x_ref, gain_ref, *out_refs):
    here = lax.axis_index("keys") // cores
    gain = gain_ref[...]
    for s in range(chips):
        values = x_ref[here ^ s].astype(f32)
        center = jnp.mean(values, axis=-1, keepdims=True)
        moved = values - center
        spread = jnp.mean(jnp.square(moved), axis=-1, keepdims=True)
        out_refs[s][...] = (moved * lax.rsqrt(spread + epsilon) * gain).astype(bf16)


def prepare(pair_rep, norm_gain, chips):
    rows, columns, channels = pair_rep.shape
    size = rows // chips
    return pl.pallas_call(
        functools.partial(prepare_kernel, chips),
        out_shape=[jax.ShapeDtypeStruct((size, columns, channels), bf16)] * chips,
        in_specs=vmem(2),
        out_specs=vmem(chips),
        name="prepare",
        compiler_params=room(kinds(pair_rep, pair_rep)),
        cost_estimate=estimate(rows * columns * channels * 12, 4 * pair_rep.size),
    )(pair_rep.reshape(chips, size, columns, channels), norm_gain.reshape(1, channels))


def stack_kernel(*refs):
    for s, ref in enumerate(refs[:-1]):
        refs[-1][s] = ref[...]


def stack(arrays):
    shape = jax.ShapeDtypeStruct((len(arrays),) + arrays[0].shape, arrays[0].dtype)
    return pl.pallas_call(
        stack_kernel,
        out_shape=shape,
        in_specs=vmem(len(arrays)),
        out_specs=pl.BlockSpec(memory_space=pltpu.VMEM),
        name="stack",
        compiler_params=room(kinds(shape, *arrays)),
        cost_estimate=estimate(arrays[0].size * 16, 4 * arrays[0].size * len(arrays)),
    )(*arrays)


def assemble_kernel(chips, pieces, *refs):
    bias_refs, out_ref = refs[:pieces], refs[pieces]
    _, head_count, columns, share = bias_refs[0].shape
    length = out_ref.shape[1]
    count = chips * columns
    me = lax.axis_index("keys")
    here, core = me // cores, me % cores
    group = lax.axis_index("rows")
    place = lax.broadcasted_iota(jnp.int32, (share, length), 1)
    first = lax.broadcasted_iota(jnp.int32, (share, length), 0)
    side, block = place // count, place // columns % chips
    key = ((here ^ block) * cores + (core ^ side)) * columns + place % columns
    picks = [(key == (group ^ t) * share + first).astype(f32).astype(bf16) for t in range(pieces)]
    for h in range(head_count):
        for s in range(chips):
            total = jnp.zeros((columns, length), f32)
            for t in range(pieces):
                total += jnp.dot(bias_refs[t][s, h], picks[t], preferred_element_type=f32)
            start = h * count + s * columns
            out_ref[start : start + columns, :] = total


def assemble(bias_pieces):
    chips, head_count, columns, share = bias_pieces[0].shape
    pieces = len(bias_pieces)
    shape = (head_count * chips * columns, pieces * share)
    return pl.pallas_call(
        functools.partial(assemble_kernel, chips, pieces),
        out_shape=jax.ShapeDtypeStruct(shape, f32),
        in_specs=vmem(pieces),
        out_specs=pl.BlockSpec(memory_space=pltpu.VMEM),
        name="assemble",
        compiler_params=room(kinds(*bias_pieces) + [(shape, f32)]),
        cost_estimate=estimate(4 * shape[0] * shape[1] * shape[1], 6 * shape[0] * shape[1]),
    )(*bias_pieces)


def hold_kernel(chips, *refs):
    own = refs[:chips]
    weights_ref, held_ref = refs[chips:]

    def step(row, carry):
        rows = jnp.concatenate([own[s][row] for s in range(chips)], axis=0)
        held_ref[row] = jnp.dot(rows, weights_ref[...], preferred_element_type=f32).astype(bf16)
        return carry

    lax.fori_loop(0, own[0].shape[0], step, 0, unroll=2)


def hold(own, weights):
    chips = len(own)
    rows, columns, channels = own[0].shape
    out = jax.ShapeDtypeStruct((rows, chips * columns, weights.shape[1]), bf16)
    return pl.pallas_call(
        functools.partial(hold_kernel, chips),
        out_shape=out,
        in_specs=vmem(chips + 1),
        out_specs=pl.BlockSpec(memory_space=pltpu.VMEM),
        name="hold",
        compiler_params=room(kinds(*own, weights, out)),
        cost_estimate=estimate(2 * out.size * channels, 4 * out.size),
    )(*own, weights)


def ask_kernel(chips, head_size, *refs):
    own, refs = refs[:chips], refs[chips:]
    weights_ref, refs = refs[0], refs[1:]
    query_refs, gate_refs = refs[:chips], refs[chips:]
    columns = own[0].shape[1]
    width = weights_ref.shape[1] // 2
    scale = head_size ** (-0.5)

    def step(row, carry):
        rows = jnp.concatenate([own[s][row] for s in range(chips)], axis=0)
        asked = jnp.dot(rows, weights_ref[...], preferred_element_type=f32)
        query = (asked[:, :width] * scale).astype(bf16)
        gate = jax.nn.sigmoid(asked[:, width:])
        for s in range(chips):
            query_refs[s][row] = query[s * columns : (s + 1) * columns]
            gate_refs[s][row] = gate[s * columns : (s + 1) * columns]
        return carry

    lax.fori_loop(0, own[0].shape[0], step, 0, unroll=2)


def ask(own, weights, head_count):
    chips = len(own)
    rows, columns, channels = own[0].shape
    width = weights.shape[1] // 2
    outs = [((rows, columns, width), kind) for kind in (bf16, f32) for _ in range(chips)]
    result = pl.pallas_call(
        functools.partial(ask_kernel, chips, width // head_count),
        out_shape=[jax.ShapeDtypeStruct(*out) for out in outs],
        in_specs=vmem(chips + 1),
        out_specs=vmem(2 * chips),
        name="ask",
        compiler_params=room(kinds(*own, weights) + outs),
        cost_estimate=estimate(4 * rows * chips * columns * channels * width, 8 * rows * chips * columns * width),
    )(*own, weights)
    return result[:chips], result[chips:]


def attend_kernel(slots, head_count, *refs):
    parts = len(slots)
    query_refs, refs = refs[:parts], refs[parts:]
    gate_refs, refs = refs[:parts], refs[parts:]
    held_ref, other_ref, bias_ref, weights_ref = refs[:4]
    out_refs, refs = refs[4 : 4 + parts], refs[4 + parts :]
    logits_a, logits_b, highest_a, highest_b, powers_a, powers_b, gated_ref = refs
    rows, columns, width = query_refs[0].shape
    length = held_ref.shape[1] * cores
    chips = held_ref.shape[1] // columns
    count = parts * columns
    lanes = highest_a.shape[1]
    ones = jnp.ones((length, width), bf16)
    lane_head = lax.broadcasted_iota(jnp.int32, (count, width), 1) // (width // head_count)

    def score(row, logits, highest):
        query = jnp.concatenate([ref[row] for ref in query_refs], axis=0)
        heads = [jnp.where(lane_head == h, query, jnp.zeros_like(query)) for h in range(head_count)]
        scores = lax.dot_general(
            jnp.concatenate(heads, axis=0),
            jnp.concatenate([held_ref[row, :, :width], other_ref[row, :, :width]], axis=0),
            (((1,), (1,)), ((), ())),
            preferred_element_type=f32,
        )
        for h in range(head_count):
            for i, s in enumerate(slots):
                part = pl.ds((h * parts + i) * columns, columns)
                start = (h * parts + i) * columns
                block = scores[start : start + columns] + bias_ref[pl.ds((h * chips + s) * columns, columns)]
                logits[part] = block
                highest[part] = jnp.broadcast_to(jnp.max(block, axis=-1, keepdims=True), (columns, lanes))

    def weigh(logits, highest, powers):
        for start in range(0, logits.shape[1], lanes):
            part = slice(start, start + lanes)
            powers[:, part] = jnp.exp(logits[:, part] - highest[...]).astype(bf16)

    def finish(row, powers):
        values = jnp.concatenate([held_ref[row, :, width:], other_ref[row, :, width:]], axis=0)
        both = jnp.dot(powers[...], jnp.concatenate([values, ones], axis=1), preferred_element_type=f32)
        summed, total = both[:count, :width], both[:count, width:]
        for h in range(1, head_count):
            part = slice(h * count, (h + 1) * count)
            summed = jnp.where(lane_head == h, both[part, :width], summed)
            total = jnp.where(lane_head == h, both[part, width:], total)
        gates = jnp.concatenate([ref[row] for ref in gate_refs], axis=0)
        gated = (gates * (summed / total)).astype(bf16)
        for i in range(parts):
            gated_ref[i, row] = gated[i * columns : (i + 1) * columns]

    def pair(step, carry):
        row = 2 * step
        score(row + 1, logits_b, highest_b)
        weigh(logits_a, highest_a, powers_a)
        if row > 0:
            finish(row - 1, powers_b)
        if row + 2 < rows:
            score(row + 2, logits_a, highest_a)
        weigh(logits_b, highest_b, powers_b)
        finish(row, powers_a)
        return carry

    score(0, logits_a, highest_a)
    for step in range(rows // 2):
        pair(step, 0)
    finish(rows - 1, powers_b)
    for i in range(parts):
        gated = gated_ref[i].reshape(rows * columns, width)
        update = jnp.dot(gated, weights_ref[...], preferred_element_type=f32).astype(bf16)
        out_refs[i][...] = update.reshape(rows, columns, width)


def attend(slots, queries, gates, held, other, bias, w_out, head_count):
    queries, gates = [queries[s] for s in slots], [gates[s] for s in slots]
    rows, columns, width = queries[0].shape
    length = held.shape[1] * cores
    stacked = head_count * len(slots) * columns
    out = jax.ShapeDtypeStruct((rows, columns, width), bf16)
    flops = rows * (stacked * length * width * 6 + 2 * len(slots) * columns * width * width)
    return pl.pallas_call(
        functools.partial(attend_kernel, slots, head_count),
        out_shape=[out] * len(slots),
        in_specs=vmem(2 * len(slots) + 4),
        out_specs=vmem(len(slots)),
        scratch_shapes=[pltpu.VMEM((stacked, length), f32)] * 2
        + [pltpu.VMEM((stacked, 128), f32)] * 2
        + [pltpu.VMEM((stacked, length), bf16)] * 2
        + [pltpu.VMEM((len(slots), rows, columns, width), bf16)],
        name="attend",
        compiler_params=room(
            kinds(*queries, *gates, held, other, bias, w_out, *([out] * len(slots)))
            + [((stacked, 2 * length + 256), f32), ((stacked, 2 * length), bf16)]
        ),
        cost_estimate=estimate(flops, 16 * rows * length * width),
    )(*queries, *gates, held, other, bias, w_out)


def place_kernel(chips, *refs):
    here = lax.axis_index("keys") // cores
    for s in range(chips):
        refs[-1][here ^ s] = refs[s][...]


def place(blocks, chips):
    size, columns, channels = blocks[0].shape
    out = pl.pallas_call(
        functools.partial(place_kernel, chips),
        out_shape=jax.ShapeDtypeStruct((chips, size, columns, channels), bf16),
        in_specs=vmem(len(blocks)),
        out_specs=pl.BlockSpec(memory_space=pltpu.VMEM),
        name="place",
        compiler_params=room(kinds(*blocks, *blocks)),
        cost_estimate=estimate(1000, 4 * size * columns * channels),
    )(*blocks)
    return out.reshape(chips * size, columns, channels)


def exchange_chips(block, s, chips):
    pairs = [(z * cores + c, (z ^ s) * cores + c) for z in range(chips) for c in range(cores)]
    return lax.ppermute(block, "keys", pairs)


def send(move, blocks):
    out = [blocks[0]]
    for s in range(1, len(blocks)):
        out.append(move(blocks[s], s))
    return out


def groups_of_slots(chips):
    half = chips // 2
    return [half, *range(1, half)], [*range(half + 1, chips), 0]


def body(chips, groups, pair_rep, norm_gain, w_query, w_key, w_value, w_gate, w_out, pair_bias):
    head_count = pair_bias.shape[0]
    along_z = lambda block, s: exchange_chips(block, s, chips)
    along_rows = lambda block, t: lax.ppermute(block, "rows", [(g, g ^ t) for g in range(groups)])
    siblings = [(i, i ^ 1) for i in range(chips * cores)]
    sent = prepare(pair_rep, norm_gain, chips)
    mine = stack(send(along_z, [pair_bias] * chips))
    bias_pieces = send(along_rows, [mine] * groups)
    own = send(along_z, sent)
    held = hold(own, jnp.concatenate([w_key, w_value], axis=1))
    other = lax.ppermute(held, "keys", siblings)
    queries, gates = ask(own, jnp.concatenate([w_query, w_gate], axis=1), head_count)
    bias = assemble(bias_pieces)
    update = [None] * chips
    for slots in groups_of_slots(chips):
        made = attend(slots, queries, gates, held, other, bias, w_out, head_count)
        for s, block in zip(slots, made):
            update[s] = block
    return place(send(along_z, update), chips)


def solution(mesh):
    placed = (P("rows", "keys", None), P(), P(), P(), P(), P(), P(), P(None, "keys", "rows"))
    chips, groups = mesh.shape["keys"] // cores, mesh.shape["rows"]
    return jax.shard_map(
        functools.partial(body, chips, groups),
        mesh=mesh,
        in_specs=placed,
        out_specs=P("rows", "keys", None),
        check_vma=False,
    )
```

profile of v0, /device:TPU:0, one launch (start us, length us, event | category | flops | bytes accessed | tf_op | source)
XLA Modules:
  0.0 58.8 jit_solution(15435811990094351689)
XLA Ops:
  0.0 1.1 %copy-done = bf16[48,48,128]{2,1,0:T(8,128)(2,1)S(1)} copy-done((bf16[48,48,128]{2,1,0:T(8,128)(2,1)S(1)}, bf16[48,48,128]{2,1,0:T(8,128)(2,1)}, u32[]{:S(2)}) %copy-start) | copy-done | bytes 589848
  1.1 0.7 %copy-done.2 = f32[128]{0:T(128)S(1)} copy-done((f32[128]{0:T(128)S(1)}, f32[128]{0:T(128)}, u32[]{:S(2)}) %copy-start.2) | copy-done | bytes 536
  1.7 0.7 %prepare.1 = (bf16[12,48,128]{2,1,0:T(8,128)(2,1)S(1)}, bf16[12,48,128]{2,1,0:T(8,128)(2,1)S(1)}, bf16[12,48,128]{2,1,0:T(8,128)(2,1)S(1)}, bf16[12,48,128]{2,1,0:T(8,128)(2,1)S(1)}) custom-call(bf16[4,12,48,128]{3,2,1,0:T(8,128)(2,1)S(1)} %bitcast.3, f32[1,128]{1,0:T(1,128)S(1)} %bitcast.4), custom_call_target="tpu_custom_call" | custom-call | flops 3538944 | bytes 1179648 | tf_op jit(solution)/shard_map/prepare/pallas_call | solution.py:49
  2.4 3.1 %collective-permute-start = (bf16[12,48,128]{2,1,0:T(8,128)(2,1)S(1)}, bf16[12,48,128]{2,1,0:T(8,128)(2,1)S(1)}, u32[]{:S(2)}, u32[]{:S(2)}) collective-permute-start(bf16[12,48,128]{2,1,0:T(8,128)(2,1)S(1)} %get-tuple-element.22), channel_id=1, source_target_pairs={{0,2},{1,3},{2,0},{3,1},{4,6},{5,7},{6,4},{7,5},{8,10},{9,11},{10,... | collective-permute-start | bytes 442376 | tf_op jit(solution)/shard_map/ppermute | solution.py:299
  5.5 2.6 %collective-permute-start.1 = (bf16[12,48,128]{2,1,0:T(8,128)(2,1)S(1)}, bf16[12,48,128]{2,1,0:T(8,128)(2,1)S(1)}, u32[]{:S(2)}, u32[]{:S(2)}) collective-permute-start(bf16[12,48,128]{2,1,0:T(8,128)(2,1)S(1)} %get-tuple-element.23), channel_id=1, source_target_pairs={{0,4},{1,5},{2,6},{3,7},{4,0},{5,1},{6,2},{7,3},{8,12},{9,13},{10,... | collective-permute-start | bytes 442376 | tf_op jit(solution)/shard_map/ppermute | solution.py:299
  8.1 0.8 %pad_maximum_fusion.1.refs_4_ = bf16[128,256]{1,0:T(8,128)(2,1)S(1)} fusion(bf16[128,128]{1,0:T(8,128)(2,1)} %param.12, bf16[128,128]{1,0:T(8,128)(2,1)} %param.11), kind=kLoop, calls=%fused_computation.1 | loop fusion | flops 131072 | bytes 131072 | tf_op jit(solution)/shard_map/concatenate | solution.py:323
  8.9 2.5 %collective-permute-done.refs_1_ = bf16[12,48,128]{2,1,0:T(8,128)(2,1)S(1)} collective-permute-done((bf16[12,48,128]{2,1,0:T(8,128)(2,1)S(1)}, bf16[12,48,128]{2,1,0:T(8,128)(2,1)S(1)}, u32[]{:S(2)}, u32[]{:S(2)}) %collective-permute-start) | collective-permute-done | bytes 147488 | tf_op jit(solution)/shard_map/ppermute | solution.py:299
  11.4 8.0 %collective-permute-done.1.refs_2_ = bf16[12,48,128]{2,1,0:T(8,128)(2,1)S(1)} collective-permute-done((bf16[12,48,128]{2,1,0:T(8,128)(2,1)S(1)}, bf16[12,48,128]{2,1,0:T(8,128)(2,1)S(1)}, u32[]{:S(2)}, u32[]{:S(2)}) %collective-permute-start.1) | collective-permute-done | bytes 147488 | tf_op jit(solution)/shard_map/ppermute | solution.py:299
  19.5 1.2 %hold.1.refs_4_ = bf16[12,192,256]{2,1,0:T(8,128)(2,1)S(1)} custom-call(bf16[12,48,128]{2,1,0:T(8,128)(2,1)S(1)} %get-tuple-element.21.refs_0_, bf16[12,48,128]{2,1,0:T(8,128)(2,1)S(1)} %collective-permute-done.refs_1_, bf16[12,48,128]{2,1,0:T(8,128)(2,1)S(1)} %collective-permute-done.1.refs_2_, bf16[12,48,128]{2,1,0:T(8,128)(2,1)S(1)} %collective-permute-done.2.refs_3_, ...), custom_call_target="tpu_custom_call" | custom-call | flops 150994944 | bytes 2359296 | tf_op jit(solution)/shard_map/hold/pallas_call | solution.py:131
  20.7 0.1 collective-permute-start.3
  20.7 3.4 %collective-permute-start.5 = (bf16[4,48,96]{2,1,0:T(8,128)(2,1)S(1)}, bf16[4,48,96]{2,1,0:T(8,128)(2,1)S(1)}, u32[]{:S(2)}, u32[]{:S(2)}) collective-permute-start(bf16[4,48,96]{2,1,0:T(8,128)(2,1)S(1)} %copy-done.1), channel_id=1, source_target_pairs={{0,4},{1,5},{2,6},{3,7},{4,0},{5,1},{6,2},{7,3},{8,12},{9,13},{10,... | collective-permute-start | bytes 110600 | tf_op jit(solution)/shard_map/ppermute | solution.py:299
  24.2 1.5 %collective-permute-start.6 = (bf16[4,48,96]{2,1,0:T(8,128)(2,1)S(1)}, bf16[4,48,96]{2,1,0:T(8,128)(2,1)S(1)}, u32[]{:S(2)}, u32[]{:S(2)}) collective-permute-start(bf16[4,48,96]{2,1,0:T(8,128)(2,1)S(1)} %copy-done.1), channel_id=1, source_target_pairs={{0,6},{1,7},{2,4},{3,5},{4,2},{5,3},{6,0},{7,1},{8,14},{9,15},{10,... | collective-permute-start | bytes 110600 | tf_op jit(solution)/shard_map/ppermute | solution.py:299
  25.7 0.8 %collective-permute-done.5.refs_2_ = bf16[4,48,96]{2,1,0:T(8,128)(2,1)S(1)} collective-permute-done((bf16[4,48,96]{2,1,0:T(8,128)(2,1)S(1)}, bf16[4,48,96]{2,1,0:T(8,128)(2,1)S(1)}, u32[]{:S(2)}, u32[]{:S(2)}) %collective-permute-start.5) | collective-permute-done | bytes 36896 | tf_op jit(solution)/shard_map/ppermute | solution.py:299
  26.5 1.8 %collective-permute-done.4.refs_1_ = bf16[4,48,96]{2,1,0:T(8,128)(2,1)S(1)} collective-permute-done((bf16[4,48,96]{2,1,0:T(8,128)(2,1)S(1)}, bf16[4,48,96]{2,1,0:T(8,128)(2,1)S(1)}, u32[]{:S(2)}, u32[]{:S(2)}) %collective-permute-start.4) | collective-permute-done | bytes 36896 | tf_op jit(solution)/shard_map/ppermute | solution.py:299
  28.3 1.8 %collective-permute-done.6.refs_3_ = bf16[4,48,96]{2,1,0:T(8,128)(2,1)S(1)} collective-permute-done((bf16[4,48,96]{2,1,0:T(8,128)(2,1)S(1)}, bf16[4,48,96]{2,1,0:T(8,128)(2,1)S(1)}, u32[]{:S(2)}, u32[]{:S(2)}) %collective-permute-start.6) | collective-permute-done | bytes 36896 | tf_op jit(solution)/shard_map/ppermute | solution.py:299
  30.1 2.5 %collective-permute-start.9 = (bf16[4,4,48,96]{3,2,1,0:T(8,128)(2,1)S(1)}, bf16[4,4,48,96]{3,2,1,0:T(8,128)(2,1)S(1)}, u32[]{:S(2)}, u32[]{:S(2)}) collective-permute-start(bf16[4,4,48,96]{3,2,1,0:T(8,128)(2,1)S(1)} %stack.1.refs_0_), channel_id=1, source_target_pairs={{0,24},{8,16},{16,8},{24,0},{1,25},{9,17},{17,9},{25,1},{2,26},{10... | collective-permute-start | bytes 442376 | tf_op jit(solution)/shard_map/ppermute | solution.py:317
  32.6 0.5 collective-permute-start.8
  33.1 0.5 collective-permute-start.7
  33.7 0.0 copy-start.3
  33.7 1.2 %ask.1 = (bf16[12,48,128]{2,1,0:T(8,128)(2,1)S(1)}, bf16[12,48,128]{2,1,0:T(8,128)(2,1)S(1)}, bf16[12,48,128]{2,1,0:T(8,128)(2,1)S(1)}, bf16[12,48,128]{2,1,0:T(...) custom-call(bf16[12,48,128]{2,1,0:T(8,128)(2,1)S(1)} %get-tuple-elem, ...), custom_call_target="tpu_custom_call" | custom-call | flops 150994944 | bytes 2359296 | tf_op jit(solution)/shard_map/ask/pallas_call | solution.py:168
  34.9 3.7 %collective-permute-done.9.refs_3_ = bf16[4,4,48,96]{3,2,1,0:T(8,128)(2,1)S(1)} collective-permute-done((bf16[4,4,48,96]{3,2,1,0:T(8,128)(2,1)S(1)}, bf16[4,4,48,96]{3,2,1,0:T(8,128)(2,1)S(1)}, u32[]{:S(2)}, u32[]{:S(2)}) %collective-permute-start.9) | collective-permute-done | bytes 147488 | tf_op jit(solution)/shard_map/ppermute | solution.py:317
  38.6 2.5 %collective-permute-done.8.refs_2_ = bf16[4,4,48,96]{3,2,1,0:T(8,128)(2,1)S(1)} collective-permute-done((bf16[4,4,48,96]{3,2,1,0:T(8,128)(2,1)S(1)}, bf16[4,4,48,96]{3,2,1,0:T(8,128)(2,1)S(1)}, u32[]{:S(2)}, u32[]{:S(2)}) %collective-permute-start.8) | collective-permute-done | bytes 147488 | tf_op jit(solution)/shard_map/ppermute | solution.py:317
  41.1 0.1 collective-permute-done.7.refs_1_
  41.2 1.0 %assemble.1.refs_6_ = f32[768,384]{1,0:T(8,128)S(1)} custom-call(bf16[4,4,48,96]{3,2,1,0:T(8,128)(2,1)S(1)} %stack.1.refs_0_, bf16[4,4,48,96]{3,2,1,0:T(8,128)(2,1)S(1)} %collective-permute-done.7.refs_1_, bf16[4,4,48,96]{3,2,1,0:T(8,128)(2,1)S(1)} %collective-permute-done.8.refs_2_, bf16[4,4,48,96]{3,2,1,0:T(8,128)(2,1)S(1)} %collective-permute-done.9.refs_3_), custom_call_target="tpu_custom_call" | custom-call | flops 452984832 | bytes 1769472 | tf_op jit(solution)/shard_map/assemble/pallas_call | solution.py:104
  42.2 2.8 %attend.3 = (bf16[12,48,128]{2,1,0:T(8,128)(2,1)S(1)}, bf16[12,48,128]{2,1,0:T(8,128)(2,1)S(1)}) custom-call(bf16[12,48,128]{2,1,0:T(8,128)(2,1)S(1)} %get-tuple-element.30.refs_0_, bf16[12,48,128]{2,1,0:T(8,128)(2,1)S(1)} %get-tuple-element.31.refs_1_, f32[12,48,128]{2,1,0:T(8,128)S(1)} %get-tuple-element.32.refs_2_, ...), custom_call_target="tpu_custom_call" | custom-call | flops 1396703232 | bytes 9437184 | tf_op jit(solution)/shard_map/attend/pallas_call | solution.py:259
  45.0 0.3 collective-permute-start.10
  45.3 2.7 %collective-permute-start.11 = (bf16[12,48,128]{2,1,0:T(8,128)(2,1)S(1)}, bf16[12,48,128]{2,1,0:T(8,128)(2,1)S(1)}, u32[]{:S(2)}, u32[]{:S(2)}) collective-permute-start(bf16[12,48,128]{2,1,0:T(8,128)(2,1)S(1)} %get-tuple-element.35), channel_id=1, source_target_pairs={{0,4},{1,5},{2,6},{3,7},{4,0},{5,1},{6,2},{7,3},{8,12},{9,13},{10,... | collective-permute-start | bytes 442376 | tf_op jit(solution)/shard_map/ppermute | solution.py:299
  48.0 2.8 %attend.2 = (bf16[12,48,128]{2,1,0:T(8,128)(2,1)S(1)}, bf16[12,48,128]{2,1,0:T(8,128)(2,1)S(1)}) custom-call(bf16[12,48,128]{2,1,0:T(8,128)(2,1)S(1)} %get-tuple-element.25.refs_0_, bf16[12,48,128]{2,1,0:T(8,128)(2,1)S(1)} %get-tuple-element.26.refs_1_, f32[12,48,128]{2,1,0:T(8,128)S(1)} %get-tuple-element.27.refs_2_, ...), custom_call_target="tpu_custom_call" | custom-call | flops 1396703232 | bytes 9437184 | tf_op jit(solution)/shard_map/attend/pallas_call | solution.py:259
  50.8 1.5 %collective-permute-start.12 = (bf16[12,48,128]{2,1,0:T(8,128)(2,1)S(1)}, bf16[12,48,128]{2,1,0:T(8,128)(2,1)S(1)}, u32[]{:S(2)}, u32[]{:S(2)}) collective-permute-start(bf16[12,48,128]{2,1,0:T(8,128)(2,1)S(1)} %get-tuple-element.36), channel_id=1, source_target_pairs={{0,6},{1,7},{2,4},{3,5},{4,2},{5,3},{6,0},{7,1},{8,14},{9,15},{10,... | collective-permute-start | bytes 442376 | tf_op jit(solution)/shard_map/ppermute | solution.py:299
  52.3 0.9 %collective-permute-done.10.refs_1_ = bf16[12,48,128]{2,1,0:T(8,128)(2,1)S(1)} collective-permute-done((bf16[12,48,128]{2,1,0:T(8,128)(2,1)S(1)}, bf16[12,48,128]{2,1,0:T(8,128)(2,1)S(1)}, u32[]{:S(2)}, u32[]{:S(2)}) %collective-permute-start.10) | collective-permute-done | bytes 147488 | tf_op jit(solution)/shard_map/ppermute | solution.py:299
  53.2 4.7 %collective-permute-done.11.refs_2_ = bf16[12,48,128]{2,1,0:T(8,128)(2,1)S(1)} collective-permute-done((bf16[12,48,128]{2,1,0:T(8,128)(2,1)S(1)}, bf16[12,48,128]{2,1,0:T(8,128)(2,1)S(1)}, u32[]{:S(2)}, u32[]{:S(2)}) %collective-permute-start.11) | collective-permute-done | bytes 147488 | tf_op jit(solution)/shard_map/ppermute | solution.py:299
  58.0 0.9 %place.1 = bf16[4,12,48,128]{3,2,1,0:T(8,128)(2,1)} custom-call(bf16[12,48,128]{2,1,0:T(8,128)(2,1)S(1)} %get-tuple-element.29.refs_0_, bf16[12,48,128]{2,1,0:T(8,128)(2,1)S(1)} %collective-permute-done.10.refs_1_, bf16[12,48,128]{2,1,0:T(8,128)(2,1)S(1)} %collective-permute-done.11.refs_2_, bf16[12,48,128]{2,1,0:T(8,128)(2,1)S(1)} %collective-permute-done.12.refs_3_), custom_call_target="tpu_custom_call" | custom-call | flops 1000 | bytes 294912 | tf_op jit(solution)/shard_map/place/pallas_call | solution.py:285
  (16 shorter events, 0.1 us)
Async XLA Ops:
  0.0 1.1 %copy-start = (bf16[48,48,128]{2,1,0:T(8,128)(2,1)S(1)}, bf16[48,48,128]{2,1,0:T(8,128)(2,1)}, u32[]{:S(2)}) copy-start(bf16[48,48,128]{2,1,0:T(8,128)(2,1)} %param.8) | copy-start | bytes 1769476
  1.1 0.7 %copy-start.2 = (f32[128]{0:T(128)S(1)}, f32[128]{0:T(128)}, u32[]{:S(2)}) copy-start(f32[128]{0:T(128)} %param.9) | copy-start | bytes 1540
  1.7 19.0 %copy-start.1 = (bf16[4,48,96]{2,1,0:T(8,128)(2,1)S(1)}, bf16[4,48,96]{2,1,0:T(8,128)(2,1)}, u32[]{:S(2)}) copy-start(bf16[4,48,96]{2,1,0:T(8,128)(2,1)} %refs_0_.1) | copy-start | bytes 110596
  2.4 9.0 %collective-permute-start = (bf16[12,48,128]{2,1,0:T(8,128)(2,1)S(1)}, bf16[12,48,128]{2,1,0:T(8,128)(2,1)S(1)}, u32[]{:S(2)}, u32[]{:S(2)}) collective-permute-start(bf16[12,48,128]{2,1,0:T(8,128)(2,1)S(1)} %get-tuple-element.22), channel_id=1, source_target_pairs={{0,2},{1,3},{2,0},{3,1},{4,6},{5,7},{6,4},{7,5},{8,10},{9,11},{10,... | collective-permute-start | bytes 442376 | tf_op jit(solution)/shard_map/ppermute | solution.py:299
  5.5 13.9 %collective-permute-start.1 = (bf16[12,48,128]{2,1,0:T(8,128)(2,1)S(1)}, bf16[12,48,128]{2,1,0:T(8,128)(2,1)S(1)}, u32[]{:S(2)}, u32[]{:S(2)}) collective-permute-start(bf16[12,48,128]{2,1,0:T(8,128)(2,1)S(1)} %get-tuple-element.23), channel_id=1, source_target_pairs={{0,4},{1,5},{2,6},{3,7},{4,0},{5,1},{6,2},{7,3},{8,12},{9,13},{10,... | collective-permute-start | bytes 442376 | tf_op jit(solution)/shard_map/ppermute | solution.py:299
  8.1 25.5 %copy-start.4 = (bf16[128,128]{1,0:T(8,128)(2,1)S(1)}, bf16[128,128]{1,0:T(8,128)(2,1)}, u32[]{:S(2)}) copy-start(bf16[128,128]{1,0:T(8,128)(2,1)} %param.13) | copy-start | bytes 98308
  8.1 25.5 %copy-start.5 = (bf16[128,128]{1,0:T(8,128)(2,1)S(1)}, bf16[128,128]{1,0:T(8,128)(2,1)}, u32[]{:S(2)}) copy-start(bf16[128,128]{1,0:T(8,128)(2,1)} %param.10) | copy-start | bytes 98308
  8.1 11.4 %collective-permute-start.2 = (bf16[12,48,128]{2,1,0:T(8,128)(2,1)S(1)}, bf16[12,48,128]{2,1,0:T(8,128)(2,1)S(1)}, u32[]{:S(2)}, u32[]{:S(2)}) collective-permute-start(bf16[12,48,128]{2,1,0:T(8,128)(2,1)S(1)} %get-tuple-element.24), channel_id=1, source_target_pairs={{0,6},{1,7},{2,4},{3,5},{4,2},{5,3},{6,0},{7,1},{8,14},{9,15},{10,... | collective-permute-start | bytes 442376 | tf_op jit(solution)/shard_map/ppermute | solution.py:299
  20.7 21.5 %collective-permute-start.3 = (bf16[12,192,256]{2,1,0:T(8,128)(2,1)S(1)}, bf16[12,192,256]{2,1,0:T(8,128)(2,1)S(1)}, u32[]{:S(2)}, u32[]{:S(2)}) collective-permute-start(bf16[12,192,256]{2,1,0:T(8,128)(2,1)S(1)} %hold.1.refs_4_), channel_id=1, source_target_pairs={{0,1},{1,0},{2,3},{3,2},{4,5},{5,4},{6,7},{7,6},{8,9},{9,8},{10,11... | collective-permute-start | bytes 3538952 | tf_op jit(solution)/shard_map/ppermute | solution.py:324
  20.7 5.8 %collective-permute-start.5 = (bf16[4,48,96]{2,1,0:T(8,128)(2,1)S(1)}, bf16[4,48,96]{2,1,0:T(8,128)(2,1)S(1)}, u32[]{:S(2)}, u32[]{:S(2)}) collective-permute-start(bf16[4,48,96]{2,1,0:T(8,128)(2,1)S(1)} %copy-done.1), channel_id=1, source_target_pairs={{0,4},{1,5},{2,6},{3,7},{4,0},{5,1},{6,2},{7,3},{8,12},{9,13},{10,... | collective-permute-start | bytes 110600 | tf_op jit(solution)/shard_map/ppermute | solution.py:299
  24.2 4.1 %collective-permute-start.4 = (bf16[4,48,96]{2,1,0:T(8,128)(2,1)S(1)}, bf16[4,48,96]{2,1,0:T(8,128)(2,1)S(1)}, u32[]{:S(2)}, u32[]{:S(2)}) collective-permute-start(bf16[4,48,96]{2,1,0:T(8,128)(2,1)S(1)} %copy-done.1), channel_id=1, source_target_pairs={{0,2},{1,3},{2,0},{3,1},{4,6},{5,7},{6,4},{7,5},{8,10},{9,11},{10,... | collective-permute-start | bytes 110600 | tf_op jit(solution)/shard_map/ppermute | solution.py:299
  24.2 5.9 %collective-permute-start.6 = (bf16[4,48,96]{2,1,0:T(8,128)(2,1)S(1)}, bf16[4,48,96]{2,1,0:T(8,128)(2,1)S(1)}, u32[]{:S(2)}, u32[]{:S(2)}) collective-permute-start(bf16[4,48,96]{2,1,0:T(8,128)(2,1)S(1)} %copy-done.1), channel_id=1, source_target_pairs={{0,6},{1,7},{2,4},{3,5},{4,2},{5,3},{6,0},{7,1},{8,14},{9,15},{10,... | collective-permute-start | bytes 110600 | tf_op jit(solution)/shard_map/ppermute | solution.py:299
  30.1 8.5 %collective-permute-start.9 = (bf16[4,4,48,96]{3,2,1,0:T(8,128)(2,1)S(1)}, bf16[4,4,48,96]{3,2,1,0:T(8,128)(2,1)S(1)}, u32[]{:S(2)}, u32[]{:S(2)}) collective-permute-start(bf16[4,4,48,96]{3,2,1,0:T(8,128)(2,1)S(1)} %stack.1.refs_0_), channel_id=1, source_target_pairs={{0,24},{8,16},{16,8},{24,0},{1,25},{9,17},{17,9},{25,1},{2,26},{10... | collective-permute-start | bytes 442376 | tf_op jit(solution)/shard_map/ppermute | solution.py:317
  32.6 8.5 %collective-permute-start.8 = (bf16[4,4,48,96]{3,2,1,0:T(8,128)(2,1)S(1)}, bf16[4,4,48,96]{3,2,1,0:T(8,128)(2,1)S(1)}, u32[]{:S(2)}, u32[]{:S(2)}) collective-permute-start(bf16[4,4,48,96]{3,2,1,0:T(8,128)(2,1)S(1)} %stack.1.refs_0_), channel_id=1, source_target_pairs={{0,16},{8,24},{16,0},{24,8},{1,17},{9,25},{17,1},{25,9},{2,18},{10... | collective-permute-start | bytes 442376 | tf_op jit(solution)/shard_map/ppermute | solution.py:317
  33.1 8.1 %collective-permute-start.7 = (bf16[4,4,48,96]{3,2,1,0:T(8,128)(2,1)S(1)}, bf16[4,4,48,96]{3,2,1,0:T(8,128)(2,1)S(1)}, u32[]{:S(2)}, u32[]{:S(2)}) collective-permute-start(bf16[4,4,48,96]{3,2,1,0:T(8,128)(2,1)S(1)} %stack.1.refs_0_), channel_id=1, source_target_pairs={{0,8},{8,0},{16,24},{24,16},{1,9},{9,1},{17,25},{25,17},{2,10},{10... | collective-permute-start | bytes 442376 | tf_op jit(solution)/shard_map/ppermute | solution.py:317
  33.7 8.5 %copy-start.3 = (bf16[128,128]{1,0:T(8,128)(2,1)S(1)}, bf16[128,128]{1,0:T(8,128)(2,1)}, u32[]{:S(2)}) copy-start(bf16[128,128]{1,0:T(8,128)(2,1)} %refs_7_.3) | copy-start | bytes 98308
  45.0 8.2 %collective-permute-start.10 = (bf16[12,48,128]{2,1,0:T(8,128)(2,1)S(1)}, bf16[12,48,128]{2,1,0:T(8,128)(2,1)S(1)}, u32[]{:S(2)}, u32[]{:S(2)}) collective-permute-start(bf16[12,48,128]{2,1,0:T(8,128)(2,1)S(1)} %get-tuple-element.34), channel_id=1, source_target_pairs={{0,2},{1,3},{2,0},{3,1},{4,6},{5,7},{6,4},{7,5},{8,10},{9,11},{10,... | collective-permute-start | bytes 442376 | tf_op jit(solution)/shard_map/ppermute | solution.py:299
  45.3 12.7 %collective-permute-start.11 = (bf16[12,48,128]{2,1,0:T(8,128)(2,1)S(1)}, bf16[12,48,128]{2,1,0:T(8,128)(2,1)S(1)}, u32[]{:S(2)}, u32[]{:S(2)}) collective-permute-start(bf16[12,48,128]{2,1,0:T(8,128)(2,1)S(1)} %get-tuple-element.35), channel_id=1, source_target_pairs={{0,4},{1,5},{2,6},{3,7},{4,0},{5,1},{6,2},{7,3},{8,12},{9,13},{10,... | collective-permute-start | bytes 442376 | tf_op jit(solution)/shard_map/ppermute | solution.py:299
  50.8 7.2 %collective-permute-start.12 = (bf16[12,48,128]{2,1,0:T(8,128)(2,1)S(1)}, bf16[12,48,128]{2,1,0:T(8,128)(2,1)S(1)}, u32[]{:S(2)}, u32[]{:S(2)}) collective-permute-start(bf16[12,48,128]{2,1,0:T(8,128)(2,1)S(1)} %get-tuple-element.36), channel_id=1, source_target_pairs={{0,6},{1,7},{2,4},{3,5},{4,2},{5,3},{6,0},{7,1},{8,14},{9,15},{10,... | collective-permute-start | bytes 442376 | tf_op jit(solution)/shard_map/ppermute | solution.py:299
where the time goes:
time: 59.8 us; the launch traced here: 58.8 us
  waiting for transfers between devices  26.8 us (45%)
  starting transfers between devices  18.8 us (31%)
  Pallas kernels  10.6 us (18%)
  local copies, waits for them, and re-layouts  1.74 us (3%)
  other arithmetic  0.8 us (1%)
    ppermute x9, waiting for transfers between devices, exchange_chips(): return lax.ppermute(block, 'keys', pairs)  20.5 us
    ppermute x9, starting transfers between devices, exchange_chips(): return lax.ppermute(block, 'keys', pairs)  15.2 us
    ppermute x3, waiting for transfers between devices, body(): lax.ppermute(block, 'rows', [(g, g ^ t) for g in range(groups)])  6.28 us
    pallas_call x2, Pallas kernels, attend(): pl.pallas_call(functools.partial(attend_kernel, slots, head_count), out_s...  5.61 us
    ppermute x3, starting transfers between devices, body(): lax.ppermute(block, 'rows', [(g, g ^ t) for g in range(groups)])  3.55 us
    unnamed x12, local copies, waits for them, and re-layouts  1.74 us
    pallas_call x1, Pallas kernels, ask(): pl.pallas_call(functools.partial(ask_kernel, chips, width // head_count),...  1.21 us
  transfers between devices with their start and end apart: 13, of which 10 were waited for; matrix products, arithmetic and copies ran while one was open for 1% of the time, Pallas kernels for 9%

commit v1 on v0

--- a/solution.py
+++ b/solution.py
@@ -53,7 +53,7 @@
         out_specs=vmem(chips),
         name="prepare",
         compiler_params=room(kinds(pair_rep, pair_rep)),
-        cost_estimate=estimate(rows * columns * channels * 12, 4 * pair_rep.size),
+        cost_estimate=estimate(rows * columns * channels * 8000, 4 * pair_rep.size),
     )(pair_rep.reshape(chips, size, columns, channels), norm_gain.reshape(1, channels))
 
 
@@ -62,79 +62,110 @@
         refs[-1][s] = ref[...]
 
 
-def stack(arrays):
-    shape = jax.ShapeDtypeStruct((len(arrays),) + arrays[0].shape, arrays[0].dtype)
+def stack(blocks):
+    shape = jax.ShapeDtypeStruct((len(blocks),) + blocks[0].shape, blocks[0].dtype)
     return pl.pallas_call(
         stack_kernel,
         out_shape=shape,
-        in_specs=vmem(len(arrays)),
+        in_specs=vmem(len(blocks)),
         out_specs=pl.BlockSpec(memory_space=pltpu.VMEM),
         name="stack",
-        compiler_params=room(kinds(shape, *arrays)),
-        cost_estimate=estimate(arrays[0].size * 16, 4 * arrays[0].size * len(arrays)),
-    )(*arrays)
-
-
-def assemble_kernel(chips, pieces, *refs):
-    bias_refs, out_ref = refs[:pieces], refs[pieces]
-    _, head_count, columns, share = bias_refs[0].shape
-    length = out_ref.shape[1]
+        compiler_params=room(kinds(shape, *blocks)),
+        cost_estimate=estimate(shape.size * 16, 4 * shape.size),
+    )(*blocks)
+
+
+def pick_kernel(pieces, chips, bias_ref, out_ref, packed_ref):
+    heads = [bias_ref[h].astype(f32) for h in range(bias_ref.shape[0])]
+    packed_ref[...] = jnp.concatenate(heads, axis=-1).astype(bf16)
+    share, length = out_ref.shape[1:]
+    columns = length // (chips * cores)
     count = chips * columns
     me = lax.axis_index("keys")
     here, core = me // cores, me % cores
     group = lax.axis_index("rows")
-    place = lax.broadcasted_iota(jnp.int32, (share, length), 1)
-    first = lax.broadcasted_iota(jnp.int32, (share, length), 0)
+    place = lax.broadcasted_iota(jnp.int32, (1, length), 1)
     side, block = place // count, place // columns % chips
     key = ((here ^ block) * cores + (core ^ side)) * columns + place % columns
-    picks = [(key == (group ^ t) * share + first).astype(f32).astype(bf16) for t in range(pieces)]
-    for h in range(head_count):
-        for s in range(chips):
-            total = jnp.zeros((columns, length), f32)
-            for t in range(pieces):
-                total += jnp.dot(bias_refs[t][s, h], picks[t], preferred_element_type=f32)
-            start = h * count + s * columns
-            out_ref[start : start + columns, :] = total
-
-
-def assemble(bias_pieces):
-    chips, head_count, columns, share = bias_pieces[0].shape
-    pieces = len(bias_pieces)
-    shape = (head_count * chips * columns, pieces * share)
-    return pl.pallas_call(
-        functools.partial(assemble_kernel, chips, pieces),
+    first = lax.broadcasted_iota(jnp.int32, (share, length), 0)
+    for t in range(pieces):
+        out_ref[t] = (first == key - (group ^ t) * share).astype(f32).astype(bf16)
+
+
+def pick(pieces, chips, pair_bias):
+    head_count, columns, share = pair_bias.shape
+    out = jax.ShapeDtypeStruct((pieces, share, pieces * share), bf16)
+    packed = jax.ShapeDtypeStruct((columns, head_count * share), bf16)
+    return pl.pallas_call(
+        functools.partial(pick_kernel, pieces, chips),
+        out_shape=[out, packed],
+        in_specs=vmem(1),
+        out_specs=vmem(2),
+        name="pick",
+        compiler_params=room(kinds(out, packed, pair_bias)),
+        cost_estimate=estimate(out.size * 16000, 2 * out.size),
+    )(pair_bias)
+
+
+def assemble_kernel(head_count, *refs):
+    bias_refs, pick_ref, out_ref = refs[:-2], refs[-2], refs[-1]
+    chips, columns, lanes = bias_refs[0].shape
+    share = lanes // head_count
+    total = None
+    for t, ref in enumerate(bias_refs):
+        piece = ref[...].reshape(chips * columns, lanes).astype(f32)
+        heads = [piece[:, h * share : (h + 1) * share] for h in range(head_count)]
+        part = jnp.dot(jnp.concatenate(heads, axis=0).astype(bf16), pick_ref[t], preferred_element_type=f32)
+        total = part if total is None else total + part
+    out_ref[...] = total
+
+
+def assemble(bias_pieces, picks, head_count):
+    chips, columns, lanes = bias_pieces[0].shape
+    shape = (head_count * chips * columns, len(bias_pieces) * lanes // head_count)
+    return pl.pallas_call(
+        functools.partial(assemble_kernel, head_count),
         out_shape=jax.ShapeDtypeStruct(shape, f32),
-        in_specs=vmem(pieces),
+        in_specs=vmem(len(bias_pieces) + 1),
         out_specs=pl.BlockSpec(memory_space=pltpu.VMEM),
         name="assemble",
-        compiler_params=room(kinds(*bias_pieces) + [(shape, f32)]),
-        cost_estimate=estimate(4 * shape[0] * shape[1] * shape[1], 6 * shape[0] * shape[1]),
-    )(*bias_pieces)
+        compiler_params=room(kinds(*bias_pieces, picks) + [(shape, f32)] * 3),
+        cost_estimate=estimate(2 * shape[0] * shape[1] * shape[1], 6 * shape[0] * shape[1]),
+    )(*bias_pieces, picks)
+
+
+def project(ref, weights):
+    rows, columns, channels = ref.shape
+    flat = ref[...].reshape(rows * columns, channels)
+    return jnp.dot(flat, weights, preferred_element_type=f32).reshape(rows, columns, weights.shape[1])
+
+
+def side_by_side(weights_ref, first):
+    width = weights_ref.shape[1]
+    parts = [weights_ref[i * width : (i + 1) * width] for i in (first, first + 1)]
+    return jnp.concatenate(parts, axis=1)
 
 
 def hold_kernel(chips, *refs):
     own = refs[:chips]
     weights_ref, held_ref = refs[chips:]
-
-    def step(row, carry):
-        rows = jnp.concatenate([own[s][row] for s in range(chips)], axis=0)
-        held_ref[row] = jnp.dot(rows, weights_ref[...], preferred_element_type=f32).astype(bf16)
-        return carry
-
-    lax.fori_loop(0, own[0].shape[0], step, 0, unroll=2)
+    weights = side_by_side(weights_ref, 0)
+    columns = own[0].shape[1]
+    for s in range(chips):
+        held_ref[:, s * columns : (s + 1) * columns] = project(own[s], weights).astype(bf16)
 
 
 def hold(own, weights):
     chips = len(own)
     rows, columns, channels = own[0].shape
-    out = jax.ShapeDtypeStruct((rows, chips * columns, weights.shape[1]), bf16)
+    out = jax.ShapeDtypeStruct((rows, chips * columns, 2 * weights.shape[1]), bf16)
     return pl.pallas_call(
         functools.partial(hold_kernel, chips),
         out_shape=out,
         in_specs=vmem(chips + 1),
         out_specs=pl.BlockSpec(memory_space=pltpu.VMEM),
         name="hold",
-        compiler_params=room(kinds(*own, weights, out)),
+        compiler_params=room(kinds(*own, weights, out, out)),
         cost_estimate=estimate(2 * out.size * channels, 4 * out.size),
     )(*own, weights)
 
@@ -143,27 +174,19 @@
     own, refs = refs[:chips], refs[chips:]
     weights_ref, refs = refs[0], refs[1:]
     query_refs, gate_refs = refs[:chips], refs[chips:]
-    columns = own[0].shape[1]
-    width = weights_ref.shape[1] // 2
+    width = weights_ref.shape[1]
+    weights = side_by_side(weights_ref, 2)
     scale = head_size ** (-0.5)
-
-    def step(row, carry):
-        rows = jnp.concatenate([own[s][row] for s in range(chips)], axis=0)
-        asked = jnp.dot(rows, weights_ref[...], preferred_element_type=f32)
-        query = (asked[:, :width] * scale).astype(bf16)
-        gate = jax.nn.sigmoid(asked[:, width:])
-        for s in range(chips):
-            query_refs[s][row] = query[s * columns : (s + 1) * columns]
-            gate_refs[s][row] = gate[s * columns : (s + 1) * columns]
-        return carry
-
-    lax.fori_loop(0, own[0].shape[0], step, 0, unroll=2)
+    for s in range(chips):
+        asked = project(own[s], weights)
+        query_refs[s][...] = (asked[:, :, :width] * scale).astype(bf16)
+        gate_refs[s][...] = jax.nn.sigmoid(asked[:, :, width:])
 
 
 def ask(own, weights, head_count):
     chips = len(own)
     rows, columns, channels = own[0].shape
-    width = weights.shape[1] // 2
+    width = weights.shape[1]
     outs = [((rows, columns, width), kind) for kind in (bf16, f32) for _ in range(chips)]
     result = pl.pallas_call(
         functools.partial(ask_kernel, chips, width // head_count),
@@ -171,22 +194,23 @@
         in_specs=vmem(chips + 1),
         out_specs=vmem(2 * chips),
         name="ask",
-        compiler_params=room(kinds(*own, weights) + outs),
+        compiler_params=room(kinds(*own, weights) + outs + outs),
         cost_estimate=estimate(4 * rows * chips * columns * channels * width, 8 * rows * chips * columns * width),
     )(*own, weights)
     return result[:chips], result[chips:]
 
 
-def attend_kernel(slots, head_count, *refs):
+def attend_kernel(slots, held_parts, head_count, *refs):
     parts = len(slots)
     query_refs, refs = refs[:parts], refs[parts:]
     gate_refs, refs = refs[:parts], refs[parts:]
-    held_ref, other_ref, bias_ref, weights_ref = refs[:4]
-    out_refs, refs = refs[4 : 4 + parts], refs[4 + parts :]
+    held_refs, refs = refs[:held_parts], refs[held_parts:]
+    bias_ref, weights_ref = refs[:2]
+    out_refs, refs = refs[2 : 2 + parts], refs[2 + parts :]
     logits_a, logits_b, highest_a, highest_b, powers_a, powers_b, gated_ref = refs
     rows, columns, width = query_refs[0].shape
-    length = held_ref.shape[1] * cores
-    chips = held_ref.shape[1] // columns
+    length = sum(ref.shape[1] for ref in held_refs)
+    chips = length // cores // columns
     count = parts * columns
     lanes = highest_a.shape[1]
     ones = jnp.ones((length, width), bf16)
@@ -197,7 +221,7 @@
         heads = [jnp.where(lane_head == h, query, jnp.zeros_like(query)) for h in range(head_count)]
         scores = lax.dot_general(
             jnp.concatenate(heads, axis=0),
-            jnp.concatenate([held_ref[row, :, :width], other_ref[row, :, :width]], axis=0),
+            jnp.concatenate([ref[row, :, :width] for ref in held_refs], axis=0),
             (((1,), (1,)), ((), ())),
             preferred_element_type=f32,
         )
@@ -215,7 +239,7 @@
             powers[:, part] = jnp.exp(logits[:, part] - highest[...]).astype(bf16)
 
     def finish(row, powers):
-        values = jnp.concatenate([held_ref[row, :, width:], other_ref[row, :, width:]], axis=0)
+        values = jnp.concatenate([ref[row, :, width:] for ref in held_refs], axis=0)
         both = jnp.dot(powers[...], jnp.concatenate([values, ones], axis=1), preferred_element_type=f32)
         summed, total = both[:count, :width], both[:count, width:]
         for h in range(1, head_count):
@@ -249,17 +273,17 @@
         out_refs[i][...] = update.reshape(rows, columns, width)
 
 
-def attend(slots, queries, gates, held, other, bias, w_out, head_count):
+def attend(slots, queries, gates, held, bias, w_out, head_count):
     queries, gates = [queries[s] for s in slots], [gates[s] for s in slots]
     rows, columns, width = queries[0].shape
-    length = held.shape[1] * cores
+    length = sum(part.shape[1] for part in held)
     stacked = head_count * len(slots) * columns
     out = jax.ShapeDtypeStruct((rows, columns, width), bf16)
     flops = rows * (stacked * length * width * 6 + 2 * len(slots) * columns * width * width)
     return pl.pallas_call(
-        functools.partial(attend_kernel, slots, head_count),
+        functools.partial(attend_kernel, slots, len(held), head_count),
         out_shape=[out] * len(slots),
-        in_specs=vmem(2 * len(slots) + 4),
+        in_specs=vmem(2 * len(slots) + len(held) + 2),
         out_specs=vmem(len(slots)),
         scratch_shapes=[pltpu.VMEM((stacked, length), f32)] * 2
         + [pltpu.VMEM((stacked, 128), f32)] * 2
@@ -267,17 +291,21 @@
         + [pltpu.VMEM((len(slots), rows, columns, width), bf16)],
         name="attend",
         compiler_params=room(
-            kinds(*queries, *gates, held, other, bias, w_out, *([out] * len(slots)))
+            kinds(*queries, *gates, *held, bias, w_out, *([out] * len(slots)))
             + [((stacked, 2 * length + 256), f32), ((stacked, 2 * length), bf16)]
         ),
         cost_estimate=estimate(flops, 16 * rows * length * width),
-    )(*queries, *gates, held, other, bias, w_out)
+    )(*queries, *gates, *held, bias, w_out)
 
 
 def place_kernel(chips, *refs):
     here = lax.axis_index("keys") // cores
-    for s in range(chips):
-        refs[-1][here ^ s] = refs[s][...]
+    out_ref, sems = refs[chips:]
+    copies = [pltpu.make_async_copy(refs[s], out_ref.at[here ^ s], sems.at[s]) for s in range(chips)]
+    for copy in copies:
+        copy.start()
+    for copy in copies:
+        copy.wait()
 
 
 def place(blocks, chips):
@@ -286,9 +314,10 @@
         functools.partial(place_kernel, chips),
         out_shape=jax.ShapeDtypeStruct((chips, size, columns, channels), bf16),
         in_specs=vmem(len(blocks)),
-        out_specs=pl.BlockSpec(memory_space=pltpu.VMEM),
+        out_specs=pl.BlockSpec(memory_space=pltpu.HBM),
+        scratch_shapes=[pltpu.SemaphoreType.DMA((chips,))],
         name="place",
-        compiler_params=room(kinds(*blocks, *blocks)),
+        compiler_params=room(kinds(*blocks)),
         cost_estimate=estimate(1000, 4 * size * columns * channels),
     )(*blocks)
     return out.reshape(chips * size, columns, channels)
@@ -316,17 +345,28 @@
     along_z = lambda block, s: exchange_chips(block, s, chips)
     along_rows = lambda block, t: lax.ppermute(block, "rows", [(g, g ^ t) for g in range(groups)])
     siblings = [(i, i ^ 1) for i in range(chips * cores)]
+    picks, mine = pick(groups, chips, pair_bias)
     sent = prepare(pair_rep, norm_gain, chips)
-    mine = stack(send(along_z, [pair_bias] * chips))
+    mine = stack(send(along_z, [mine] * chips))
     bias_pieces = send(along_rows, [mine] * groups)
     own = send(along_z, sent)
-    held = hold(own, jnp.concatenate([w_key, w_value], axis=1))
-    other = lax.ppermute(held, "keys", siblings)
-    queries, gates = ask(own, jnp.concatenate([w_query, w_gate], axis=1), head_count)
-    bias = assemble(bias_pieces)
+    weights = jnp.concatenate([w_key, w_value, w_query, w_gate], axis=0)
+    cross = lambda block: lax.ppermute(block, "keys", siblings)
+    early, late = own[: chips // 2], own[chips // 2 :]
+    held = [hold(early, weights)]
+    other = [cross(held[0])]
+    queries, gates = ask(early, weights, head_count)
+    crossed = []
+    for block in late:
+        crossed.append(cross(block))
+    held.append(hold(late, weights))
+    asked = ask(late, weights, head_count)
+    queries, gates = queries + asked[0], gates + asked[1]
+    other.append(hold(crossed, weights))
+    bias = assemble(bias_pieces, picks, head_count)
     update = [None] * chips
     for slots in groups_of_slots(chips):
-        made = attend(slots, queries, gates, held, other, bias, w_out, head_count)
+        made = attend(slots, queries, gates, held + other, bias, w_out, head_count)
         for s, block in zip(slots, made):
             update[s] = block
     return place(send(along_z, update), chips)

time: 59.8 us -> 52 us (0.87); the launches traced: 58.8 us -> 51.7 us
  waiting for transfers between devices: 26.8 us -> 17.4 us
  starting transfers between devices: 18.8 us -> 22.7 us
  Pallas kernels: 10.6 us -> 9.58 us
  other arithmetic: 0.8 us -> 0 us
    ppermute x9, waiting for transfers between devices: 20.5 us -> 15.2 us  [exchange_chips(): return lax.ppermute(block, 'keys', pairs)]
    ppermute x3, waiting for transfers between devices: 6.28 us -> 2.22 us  [body(): lax.ppermute(block, 'rows', [(g, g ^ t) for g in range(groups)])]
    ppermute x9, starting transfers between devices: 15.2 us -> 17.6 us  [exchange_chips(): return lax.ppermute(block, 'keys', pairs)]
    ppermute x3, starting transfers between devices: 3.55 us -> 4.53 us  [body(): lax.ppermute(block, 'rows', [(g, g ^ t) for g in range(groups)])]
    concatenate x2 -> x0, other arithmetic: 0.8 us -> none  [the longest x1 0.8 us: body(): held = hold(own, jnp.concatenate([w_key, w_value], axis=1))]
    pallas_call x1 -> x2, Pallas kernels: 1.21 us -> 0.6 us  [ask(): pl.pallas_call(functools.partial(ask_kernel, chips, width // head_count),...]
    pallas_call x4 -> x5, Pallas kernels: 6.63 us -> 6.54 us  [the longest x2 5.61 us: attend(): pl.pallas_call(functools.partial(attend_kernel, slots, len(held), head_co...]
    unnamed x12 -> x19, local copies, waits for them, and re-layouts: 1.74 us -> 1.77 us
  transfers between devices with their start and end apart: 13 -> 15, of which waited for: 10 -> 6; matrix products, arithmetic and copies ran while one was open for 1% -> 0% of each run, Pallas kernels for 9% -> 10%
where the time goes in v1:
time: 52 us; the launch traced here: 51.7 us
  starting transfers between devices  22.7 us (44%)
  waiting for transfers between devices  17.4 us (33%)
  Pallas kernels  9.58 us (18%)
  local copies, waits for them, and re-layouts  1.78 us (3%)
    ppermute x9, starting transfers between devices, exchange_chips(): return lax.ppermute(block, 'keys', pairs)  17.6 us
    ppermute x9, waiting for transfers between devices, exchange_chips(): return lax.ppermute(block, 'keys', pairs)  15.2 us
    pallas_call x2, Pallas kernels, attend(): pl.pallas_call(functools.partial(attend_kernel, slots, len(held), head_co...  5.61 us
    ppermute x3, starting transfers between devices, body(): lax.ppermute(block, 'rows', [(g, g ^ t) for g in range(groups)])  4.53 us
    ppermute x3, waiting for transfers between devices, body(): lax.ppermute(block, 'rows', [(g, g ^ t) for g in range(groups)])  2.22 us
    unnamed x19, local copies, waits for them, and re-layouts  1.77 us
  transfers between devices with their start and end apart: 15, of which 6 were waited for; matrix products, arithmetic and copies ran while one was open for 0% of the time, Pallas kernels for 10%

profile of v1, /device:TPU:0, one launch (start us, length us, event | category | flops | bytes accessed | tf_op | source)
XLA Modules:
  0.0 51.7 jit_solution(5547598776449816052)
XLA Ops:
  0.0 1.1 %copy-done = bf16[48,48,128]{2,1,0:T(8,128)(2,1)S(1)} copy-done((bf16[48,48,128]{2,1,0:T(8,128)(2,1)S(1)}, bf16[48,48,128]{2,1,0:T(8,128)(2,1)}, u32[]{:S(2)}) %copy-start) | copy-done | bytes 589848
  1.1 0.7 %copy-done.3 = f32[128]{0:T(128)S(1)} copy-done((f32[128]{0:T(128)S(1)}, f32[128]{0:T(128)}, u32[]{:S(2)}) %copy-start.3) | copy-done | bytes 536
  1.7 0.7 %prepare.1 = (bf16[12,48,128]{2,1,0:T(8,128)(2,1)S(1)}, bf16[12,48,128]{2,1,0:T(8,128)(2,1)S(1)}, bf16[12,48,128]{2,1,0:T(8,128)(2,1)S(1)}, bf16[12,48,128]{2,1,0:T(8,128)(2,1)S(1)}) custom-call(bf16[4,12,48,128]{3,2,1,0:T(8,128)(2,1)S(1)} %bitcast.3, f32[1,128]{1,0:T(1,128)S(1)} %bitcast.4), custom_call_target="tpu_custom_call" | custom-call | flops 2359296000 | bytes 1179648 | tf_op jit(solution)/shard_map/prepare/pallas_call | solution.py:49
  2.5 3.1 %collective-permute-start.2 = (bf16[12,48,128]{2,1,0:T(8,128)(2,1)S(1)}, bf16[12,48,128]{2,1,0:T(8,128)(2,1)S(1)}, u32[]{:S(2)}, u32[]{:S(2)}) collective-permute-start(bf16[12,48,128]{2,1,0:T(8,128)(2,1)S(1)} %get-tuple-element.27), channel_id=1, source_target_pairs={{0,2},{1,3},{2,0},{3,1},{4,6},{5,7},{6,4},{7,5},{8,10},{9,11},{10,... | collective-permute-start | bytes 442376 | tf_op jit(solution)/shard_map/ppermute | solution.py:328
  5.7 3.8 %collective-permute-done.2.refs_1_ = bf16[12,48,128]{2,1,0:T(8,128)(2,1)S(1)} collective-permute-done((bf16[12,48,128]{2,1,0:T(8,128)(2,1)S(1)}, bf16[12,48,128]{2,1,0:T(8,128)(2,1)S(1)}, u32[]{:S(2)}, u32[]{:S(2)}) %collective-permute-start.2) | collective-permute-done | bytes 147488 | tf_op jit(solution)/shard_map/ppermute | solution.py:328
  9.4 0.3 hold.3.refs_4_
  9.7 0.1 collective-permute-start.3
  9.8 0.1 pick.1
  10.0 3.8 %collective-permute-start.8 = (bf16[48,384]{1,0:T(8,128)(2,1)S(1)}, bf16[48,384]{1,0:T(8,128)(2,1)S(1)}, u32[]{:S(2)}, u32[]{:S(2)}) collective-permute-start(bf16[48,384]{1,0:T(8,128)(2,1)S(1)} %get-tuple-element.31.refs_0_), channel_id=1, source_target_pairs={{0,6},{1,7},{2,4},{3,5},{4,2},{5,3},{6,0},{7,1},{8,14},{9,15},{10,... | collective-permute-start | bytes 110600 | tf_op jit(solution)/shard_map/ppermute | solution.py:328
  13.8 0.6 %collective-permute-start.6 = (bf16[48,384]{1,0:T(8,128)(2,1)S(1)}, bf16[48,384]{1,0:T(8,128)(2,1)S(1)}, u32[]{:S(2)}, u32[]{:S(2)}) collective-permute-start(bf16[48,384]{1,0:T(8,128)(2,1)S(1)} %get-tuple-element.31.refs_0_), channel_id=1, source_target_pairs={{0,2},{1,3},{2,0},{3,1},{4,6},{5,7},{6,4},{7,5},{8,10},{9,11},{10,... | collective-permute-start | bytes 110600 | tf_op jit(solution)/shard_map/ppermute | solution.py:328
  14.4 2.3 %collective-permute-start = (bf16[12,48,128]{2,1,0:T(8,128)(2,1)S(1)}, bf16[12,48,128]{2,1,0:T(8,128)(2,1)S(1)}, u32[]{:S(2)}, u32[]{:S(2)}) collective-permute-start(bf16[12,48,128]{2,1,0:T(8,128)(2,1)S(1)} %get-tuple-element.23), channel_id=1, source_target_pairs={{0,4},{1,5},{2,6},{3,7},{4,0},{5,1},{6,2},{7,3},{8,12},{9,13},{10,... | collective-permute-start | bytes 442376 | tf_op jit(solution)/shard_map/ppermute | solution.py:328
  16.7 3.2 %collective-permute-start.1 = (bf16[12,48,128]{2,1,0:T(8,128)(2,1)S(1)}, bf16[12,48,128]{2,1,0:T(8,128)(2,1)S(1)}, u32[]{:S(2)}, u32[]{:S(2)}) collective-permute-start(bf16[12,48,128]{2,1,0:T(8,128)(2,1)S(1)} %get-tuple-element.24), channel_id=1, source_target_pairs={{0,6},{1,7},{2,4},{3,5},{4,2},{5,3},{6,0},{7,1},{8,14},{9,15},{10,... | collective-permute-start | bytes 442376 | tf_op jit(solution)/shard_map/ppermute | solution.py:328
  20.0 2.5 %collective-permute-start.11 = (bf16[4,48,384]{2,1,0:T(8,128)(2,1)S(1)}, bf16[4,48,384]{2,1,0:T(8,128)(2,1)S(1)}, u32[]{:S(2)}, u32[]{:S(2)}) collective-permute-start(bf16[4,48,384]{2,1,0:T(8,128)(2,1)S(1)} %stack.1.refs_0_), channel_id=1, source_target_pairs={{0,24},{8,16},{16,8},{24,0},{1,25},{9,17},{17,9},{25,1},{2,26},{10... | collective-permute-start | bytes 442376 | tf_op jit(solution)/shard_map/ppermute | solution.py:346
  22.5 0.5 collective-permute-start.10
  23.0 5.5 %collective-permute-done.refs_0_ = bf16[12,48,128]{2,1,0:T(8,128)(2,1)S(1)} collective-permute-done((bf16[12,48,128]{2,1,0:T(8,128)(2,1)S(1)}, bf16[12,48,128]{2,1,0:T(8,128)(2,1)S(1)}, u32[]{:S(2)}, u32[]{:S(2)}) %collective-permute-start) | collective-permute-done | bytes 147488 | tf_op jit(solution)/shard_map/ppermute | solution.py:328
  28.6 1.5 %collective-permute-start.9 = (bf16[4,48,384]{2,1,0:T(8,128)(2,1)S(1)}, bf16[4,48,384]{2,1,0:T(8,128)(2,1)S(1)}, u32[]{:S(2)}, u32[]{:S(2)}) collective-permute-start(bf16[4,48,384]{2,1,0:T(8,128)(2,1)S(1)} %stack.1.refs_0_), channel_id=1, source_target_pairs={{0,8},{8,0},{16,24},{24,16},{1,9},{9,1},{17,25},{25,17},{2,10},{10... | collective-permute-start | bytes 442376 | tf_op jit(solution)/shard_map/ppermute | solution.py:346
  30.1 0.5 collective-permute-start.5
  30.6 0.3 hold.4.refs_5_
  30.9 0.3 ask.2
  31.2 0.3 ask.3
  31.5 2.2 %collective-permute-done.9.refs_1_ = bf16[4,48,384]{2,1,0:T(8,128)(2,1)S(1)} collective-permute-done((bf16[4,48,384]{2,1,0:T(8,128)(2,1)S(1)}, bf16[4,48,384]{2,1,0:T(8,128)(2,1)S(1)}, u32[]{:S(2)}, u32[]{:S(2)}) %collective-permute-start.9) | collective-permute-done | bytes 147488 | tf_op jit(solution)/shard_map/ppermute | solution.py:346
  33.7 0.8 %assemble.1.refs_8_ = f32[768,384]{1,0:T(8,128)S(1)} custom-call(bf16[4,48,384]{2,1,0:T(8,128)(2,1)S(1)} %stack.1.refs_0_, bf16[4,48,384]{2,1,0:T(8,128)(2,1)S(1)} %collective-permute-done.9.refs_1_, bf16[4,48,384]{2,1,0:T(8,128)(2,1)S(1)} %collective-permute-done.10.refs_2_, bf16[4,48,384]{2,1,0:T(8,128)(2,1)S(1)} %collective-permute-done.11.refs_3_, ...), custom_call_target="tpu_custom_call" | custom-call | flops 226492416 | bytes 1769472 | tf_op jit(solution)/shard_map/assemble/pallas_call | solution.py:126
  34.5 0.3 hold.5.refs_7_
  34.8 2.8 %attend.3 = (bf16[12,48,128]{2,1,0:T(8,128)(2,1)S(1)}, bf16[12,48,128]{2,1,0:T(8,128)(2,1)S(1)}) custom-call(bf16[12,48,128]{2,1,0:T(8,128)(2,1)S(1)} %get-tuple-element.34.refs_0_, bf16[12,48,128]{2,1,0:T(8,128)(2,1)S(1)} %get-tuple-element.35.refs_1_, f32[12,48,128]{2,1,0:T(8,128)S(1)} %get-tuple-element.36.refs_2_, ...), custom_call_target="tpu_custom_call" | custom-call | flops 1396703232 | bytes 9437184 | tf_op jit(solution)/shard_map/attend/pallas_call | solution.py:283
  37.7 0.1 collective-permute-start.12
  37.7 3.2 %collective-permute-start.13 = (bf16[12,48,128]{2,1,0:T(8,128)(2,1)S(1)}, bf16[12,48,128]{2,1,0:T(8,128)(2,1)S(1)}, u32[]{:S(2)}, u32[]{:S(2)}) collective-permute-start(bf16[12,48,128]{2,1,0:T(8,128)(2,1)S(1)} %get-tuple-element.39), channel_id=1, source_target_pairs={{0,4},{1,5},{2,6},{3,7},{4,0},{5,1},{6,2},{7,3},{8,12},{9,13},{10,... | collective-permute-start | bytes 442376 | tf_op jit(solution)/shard_map/ppermute | solution.py:328
  40.9 2.8 %attend.2 = (bf16[12,48,128]{2,1,0:T(8,128)(2,1)S(1)}, bf16[12,48,128]{2,1,0:T(8,128)(2,1)S(1)}) custom-call(bf16[12,48,128]{2,1,0:T(8,128)(2,1)S(1)} %get-tuple-element.25.refs_0_, bf16[12,48,128]{2,1,0:T(8,128)(2,1)S(1)} %get-tuple-element.28.refs_1_, f32[12,48,128]{2,1,0:T(8,128)S(1)} %get-tuple-element.29.refs_2_, ...), custom_call_target="tpu_custom_call" | custom-call | flops 1396703232 | bytes 9437184 | tf_op jit(solution)/shard_map/attend/pallas_call | solution.py:283
  43.7 1.2 %collective-permute-start.14 = (bf16[12,48,128]{2,1,0:T(8,128)(2,1)S(1)}, bf16[12,48,128]{2,1,0:T(8,128)(2,1)S(1)}, u32[]{:S(2)}, u32[]{:S(2)}) collective-permute-start(bf16[12,48,128]{2,1,0:T(8,128)(2,1)S(1)} %get-tuple-element.40), channel_id=1, source_target_pairs={{0,6},{1,7},{2,4},{3,5},{4,2},{5,3},{6,0},{7,1},{8,14},{9,15},{10,... | collective-permute-start | bytes 442376 | tf_op jit(solution)/shard_map/ppermute | solution.py:328
  45.0 0.1 collective-permute-done.12.refs_1_
  45.1 3.9 %collective-permute-done.13.refs_2_ = bf16[12,48,128]{2,1,0:T(8,128)(2,1)S(1)} collective-permute-done((bf16[12,48,128]{2,1,0:T(8,128)(2,1)S(1)}, bf16[12,48,128]{2,1,0:T(8,128)(2,1)S(1)}, u32[]{:S(2)}, u32[]{:S(2)}) %collective-permute-start.13) | collective-permute-done | bytes 147488 | tf_op jit(solution)/shard_map/ppermute | solution.py:328
  49.0 1.9 %collective-permute-done.14.refs_3_ = bf16[12,48,128]{2,1,0:T(8,128)(2,1)S(1)} collective-permute-done((bf16[12,48,128]{2,1,0:T(8,128)(2,1)S(1)}, bf16[12,48,128]{2,1,0:T(8,128)(2,1)S(1)}, u32[]{:S(2)}, u32[]{:S(2)}) %collective-permute-start.14) | collective-permute-done | bytes 147488 | tf_op jit(solution)/shard_map/ppermute | solution.py:328
  50.9 0.8 %place.1 = bf16[4,12,48,128]{3,2,1,0:T(8,128)(2,1)} custom-call(bf16[12,48,128]{2,1,0:T(8,128)(2,1)S(1)} %get-tuple-element.33.refs_0_, bf16[12,48,128]{2,1,0:T(8,128)(2,1)S(1)} %collective-permute-done.12.refs_1_, bf16[12,48,128]{2,1,0:T(8,128)(2,1)S(1)} %collective-permute-done.13.refs_2_, bf16[12,48,128]{2,1,0:T(8,128)(2,1)S(1)} %collective-permute-done.14.refs_3_), custom_call_target="tpu_custom_call" | custom-call | flops 1000 | bytes 294912 | tf_op jit(solution)/shard_map/place/pallas_call | solution.py:313
  (30 shorter events, 0.1 us)
Async XLA Ops:
  0.0 1.1 %copy-start = (bf16[48,48,128]{2,1,0:T(8,128)(2,1)S(1)}, bf16[48,48,128]{2,1,0:T(8,128)(2,1)}, u32[]{:S(2)}) copy-start(bf16[48,48,128]{2,1,0:T(8,128)(2,1)} %param.8) | copy-start | bytes 1769476
  1.1 0.7 %copy-start.3 = (f32[128]{0:T(128)S(1)}, f32[128]{0:T(128)}, u32[]{:S(2)}) copy-start(f32[128]{0:T(128)} %param.9) | copy-start | bytes 1540
  1.7 3.9 %copy-start.4 = (bf16[128,128]{1,0:T(8,128)(2,1)S(1)}, bf16[128,128]{1,0:T(8,128)(2,1)}, u32[]{:S(2)}) copy-start(bf16[128,128]{1,0:T(8,128)(2,1)} %param.11) | copy-start | bytes 98308
  1.7 3.9 %copy-start.5 = (bf16[128,128]{1,0:T(8,128)(2,1)S(1)}, bf16[128,128]{1,0:T(8,128)(2,1)}, u32[]{:S(2)}) copy-start(bf16[128,128]{1,0:T(8,128)(2,1)} %param.12) | copy-start | bytes 98308
  1.7 3.9 %copy-start.6 = (bf16[128,128]{1,0:T(8,128)(2,1)S(1)}, bf16[128,128]{1,0:T(8,128)(2,1)}, u32[]{:S(2)}) copy-start(bf16[128,128]{1,0:T(8,128)(2,1)} %param.10) | copy-start | bytes 98308
  1.7 3.9 %copy-start.7 = (bf16[128,128]{1,0:T(8,128)(2,1)S(1)}, bf16[128,128]{1,0:T(8,128)(2,1)}, u32[]{:S(2)}) copy-start(bf16[128,128]{1,0:T(8,128)(2,1)} %param.13) | copy-start | bytes 98308
  2.5 7.4 %copy-start.1 = (bf16[4,48,96]{2,1,0:T(8,128)(2,1)S(1)}, bf16[4,48,96]{2,1,0:T(8,128)(2,1)}, u32[]{:S(2)}) copy-start(bf16[4,48,96]{2,1,0:T(8,128)(2,1)} %bias_ref.1) | copy-start | bytes 110596
  2.5 7.0 %collective-permute-start.2 = (bf16[12,48,128]{2,1,0:T(8,128)(2,1)S(1)}, bf16[12,48,128]{2,1,0:T(8,128)(2,1)S(1)}, u32[]{:S(2)}, u32[]{:S(2)}) collective-permute-start(bf16[12,48,128]{2,1,0:T(8,128)(2,1)S(1)} %get-tuple-element.27), channel_id=1, source_target_pairs={{0,2},{1,3},{2,0},{3,1},{4,6},{5,7},{6,4},{7,5},{8,10},{9,11},{10,... | collective-permute-start | bytes 442376 | tf_op jit(solution)/shard_map/ppermute | solution.py:328
  9.7 25.1 %collective-permute-start.3 = (bf16[12,96,256]{2,1,0:T(8,128)(2,1)S(1)}, bf16[12,96,256]{2,1,0:T(8,128)(2,1)S(1)}, u32[]{:S(2)}, u32[]{:S(2)}) collective-permute-start(bf16[12,96,256]{2,1,0:T(8,128)(2,1)S(1)} %hold.3.refs_4_), channel_id=1, source_target_pairs={{0,1},{1,0},{2,3},{3,2},{4,5},{5,4},{6,7},{7,6},{8,9},{9,8},{10,11... | collective-permute-start | bytes 1769480 | tf_op jit(solution)/shard_map/ppermute | solution.py:354
  10.0 6.8 %collective-permute-start.8 = (bf16[48,384]{1,0:T(8,128)(2,1)S(1)}, bf16[48,384]{1,0:T(8,128)(2,1)S(1)}, u32[]{:S(2)}, u32[]{:S(2)}) collective-permute-start(bf16[48,384]{1,0:T(8,128)(2,1)S(1)} %get-tuple-element.31.refs_0_), channel_id=1, source_target_pairs={{0,6},{1,7},{2,4},{3,5},{4,2},{5,3},{6,0},{7,1},{8,14},{9,15},{10,... | collective-permute-start | bytes 110600 | tf_op jit(solution)/shard_map/ppermute | solution.py:328
  13.8 6.2 %collective-permute-start.7 = (bf16[48,384]{1,0:T(8,128)(2,1)S(1)}, bf16[48,384]{1,0:T(8,128)(2,1)S(1)}, u32[]{:S(2)}, u32[]{:S(2)}) collective-permute-start(bf16[48,384]{1,0:T(8,128)(2,1)S(1)} %get-tuple-element.31.refs_0_), channel_id=1, source_target_pairs={{0,4},{1,5},{2,6},{3,7},{4,0},{5,1},{6,2},{7,3},{8,12},{9,13},{10,... | collective-permute-start | bytes 110600 | tf_op jit(solution)/shard_map/ppermute | solution.py:328
  13.8 6.2 %collective-permute-start.6 = (bf16[48,384]{1,0:T(8,128)(2,1)S(1)}, bf16[48,384]{1,0:T(8,128)(2,1)S(1)}, u32[]{:S(2)}, u32[]{:S(2)}) collective-permute-start(bf16[48,384]{1,0:T(8,128)(2,1)S(1)} %get-tuple-element.31.refs_0_), channel_id=1, source_target_pairs={{0,2},{1,3},{2,0},{3,1},{4,6},{5,7},{6,4},{7,5},{8,10},{9,11},{10,... | collective-permute-start | bytes 110600 | tf_op jit(solution)/shard_map/ppermute | solution.py:328
  14.4 14.1 %collective-permute-start = (bf16[12,48,128]{2,1,0:T(8,128)(2,1)S(1)}, bf16[12,48,128]{2,1,0:T(8,128)(2,1)S(1)}, u32[]{:S(2)}, u32[]{:S(2)}) collective-permute-start(bf16[12,48,128]{2,1,0:T(8,128)(2,1)S(1)} %get-tuple-element.23), channel_id=1, source_target_pairs={{0,4},{1,5},{2,6},{3,7},{4,0},{5,1},{6,2},{7,3},{8,12},{9,13},{10,... | collective-permute-start | bytes 442376 | tf_op jit(solution)/shard_map/ppermute | solution.py:328
  16.7 13.3 %collective-permute-start.1 = (bf16[12,48,128]{2,1,0:T(8,128)(2,1)S(1)}, bf16[12,48,128]{2,1,0:T(8,128)(2,1)S(1)}, u32[]{:S(2)}, u32[]{:S(2)}) collective-permute-start(bf16[12,48,128]{2,1,0:T(8,128)(2,1)S(1)} %get-tuple-element.24), channel_id=1, source_target_pairs={{0,6},{1,7},{2,4},{3,5},{4,2},{5,3},{6,0},{7,1},{8,14},{9,15},{10,... | collective-permute-start | bytes 442376 | tf_op jit(solution)/shard_map/ppermute | solution.py:328
  20.0 10.1 %collective-permute-start.11 = (bf16[4,48,384]{2,1,0:T(8,128)(2,1)S(1)}, bf16[4,48,384]{2,1,0:T(8,128)(2,1)S(1)}, u32[]{:S(2)}, u32[]{:S(2)}) collective-permute-start(bf16[4,48,384]{2,1,0:T(8,128)(2,1)S(1)} %stack.1.refs_0_), channel_id=1, source_target_pairs={{0,24},{8,16},{16,8},{24,0},{1,25},{9,17},{17,9},{25,1},{2,26},{10... | collective-permute-start | bytes 442376 | tf_op jit(solution)/shard_map/ppermute | solution.py:346
  22.5 9.0 %collective-permute-start.10 = (bf16[4,48,384]{2,1,0:T(8,128)(2,1)S(1)}, bf16[4,48,384]{2,1,0:T(8,128)(2,1)S(1)}, u32[]{:S(2)}, u32[]{:S(2)}) collective-permute-start(bf16[4,48,384]{2,1,0:T(8,128)(2,1)S(1)} %stack.1.refs_0_), channel_id=1, source_target_pairs={{0,16},{8,24},{16,0},{24,8},{1,17},{9,25},{17,1},{25,9},{2,18},{10... | collective-permute-start | bytes 442376 | tf_op jit(solution)/shard_map/ppermute | solution.py:346
  28.6 5.1 %collective-permute-start.9 = (bf16[4,48,384]{2,1,0:T(8,128)(2,1)S(1)}, bf16[4,48,384]{2,1,0:T(8,128)(2,1)S(1)}, u32[]{:S(2)}, u32[]{:S(2)}) collective-permute-start(bf16[4,48,384]{2,1,0:T(8,128)(2,1)S(1)} %stack.1.refs_0_), channel_id=1, source_target_pairs={{0,8},{8,0},{16,24},{24,16},{1,9},{9,1},{17,25},{25,17},{2,10},{10... | collective-permute-start | bytes 442376 | tf_op jit(solution)/shard_map/ppermute | solution.py:346
  30.0 4.5 %collective-permute-start.4 = (bf16[12,48,128]{2,1,0:T(8,128)(2,1)S(1)}, bf16[12,48,128]{2,1,0:T(8,128)(2,1)S(1)}, u32[]{:S(2)}, u32[]{:S(2)}) collective-permute-start(bf16[12,48,128]{2,1,0:T(8,128)(2,1)S(1)} %collective-permute-done.refs_0_), channel_id=1, source_target_pairs={{0,1},{1,0},{2,3},{3,2},{4,5},{5,4},{6,7},{7,6},{8,9},{9,8},{10,11... | collective-permute-start | bytes 442376 | tf_op jit(solution)/shard_map/ppermute | solution.py:354
  30.1 4.5 %collective-permute-start.5 = (bf16[12,48,128]{2,1,0:T(8,128)(2,1)S(1)}, bf16[12,48,128]{2,1,0:T(8,128)(2,1)S(1)}, u32[]{:S(2)}, u32[]{:S(2)}) collective-permute-start(bf16[12,48,128]{2,1,0:T(8,128)(2,1)S(1)} %collective-permute-done.1.refs_1_), channel_id=1, source_target_pairs={{0,1},{1,0},{2,3},{3,2},{4,5},{5,4},{6,7},{7,6},{8,9},{9,8},{10,11... | collective-permute-start | bytes 442376 | tf_op jit(solution)/shard_map/ppermute | solution.py:354
  33.7 1.1 %copy-start.2 = (bf16[128,128]{1,0:T(8,128)(2,1)S(1)}, bf16[128,128]{1,0:T(8,128)(2,1)}, u32[]{:S(2)}) copy-start(bf16[128,128]{1,0:T(8,128)(2,1)} %refs_9_.3) | copy-start | bytes 98308
  37.7 7.4 %collective-permute-start.12 = (bf16[12,48,128]{2,1,0:T(8,128)(2,1)S(1)}, bf16[12,48,128]{2,1,0:T(8,128)(2,1)S(1)}, u32[]{:S(2)}, u32[]{:S(2)}) collective-permute-start(bf16[12,48,128]{2,1,0:T(8,128)(2,1)S(1)} %get-tuple-element.38), channel_id=1, source_target_pairs={{0,2},{1,3},{2,0},{3,1},{4,6},{5,7},{6,4},{7,5},{8,10},{9,11},{10,... | collective-permute-start | bytes 442376 | tf_op jit(solution)/shard_map/ppermute | solution.py:328
  37.7 11.3 %collective-permute-start.13 = (bf16[12,48,128]{2,1,0:T(8,128)(2,1)S(1)}, bf16[12,48,128]{2,1,0:T(8,128)(2,1)S(1)}, u32[]{:S(2)}, u32[]{:S(2)}) collective-permute-start(bf16[12,48,128]{2,1,0:T(8,128)(2,1)S(1)} %get-tuple-element.39), channel_id=1, source_target_pairs={{0,4},{1,5},{2,6},{3,7},{4,0},{5,1},{6,2},{7,3},{8,12},{9,13},{10,... | collective-permute-start | bytes 442376 | tf_op jit(solution)/shard_map/ppermute | solution.py:328
  43.7 7.1 %collective-permute-start.14 = (bf16[12,48,128]{2,1,0:T(8,128)(2,1)S(1)}, bf16[12,48,128]{2,1,0:T(8,128)(2,1)S(1)}, u32[]{:S(2)}, u32[]{:S(2)}) collective-permute-start(bf16[12,48,128]{2,1,0:T(8,128)(2,1)S(1)} %get-tuple-element.40), channel_id=1, source_target_pairs={{0,6},{1,7},{2,4},{3,5},{4,2},{5,3},{6,0},{7,1},{8,14},{9,15},{10,... | collective-permute-start | bytes 442376 | tf_op jit(solution)/shard_map/ppermute | solution.py:328
